TPU v7x, 32 devices: a whole 2x2x4 slice. The times are simulated.
32 devices in a mesh: row: 16 (over z, x, core), ch: 2 (over y).
Axes of the slice: x: 2, y: 2, z: 4, core: 2. Of those that a mesh axis runs over, the one named last changes fastest.
Arguments:
- pair_rep: float32 [256, 256, 128], P('row', 'ch'), may hold values from -6 to 6
- residue_mask: int32 [256], replicated, may hold values 0 or 1
- pair_gain: float32 [2, 128], replicated, may hold values from 0.5 to 1.5
- pair_shift: float32 [2, 128], replicated, may hold values from -3 to 3
- panel_weight: bfloat16 [2, 128, 512], replicated, may hold values from -0.5 to 0.5
- panel_bias: float32 [2, 512], replicated, may hold values from -3 to 3
- gate_weight: bfloat16 [2, 128, 128], replicated, may hold values from -0.5 to 0.5
- gate_bias: float32 [2, 128], replicated, may hold values from -3 to 3
- hidden_gain: float32 [2, 128], replicated, may hold values from 0.5 to 1.5
- hidden_shift: float32 [2, 128], replicated, may hold values from -3 to 3
- output_weight: bfloat16 [2, 128, 128], replicated, may hold values from -0.5 to 0.5
- output_bias: float32 [2, 128], replicated, may hold values from -3 to 3
Outputs:
- updated_pair: float32 [256, 256, 128], P('row', 'ch')
All inputs are finite; a program needn't handle non-finite values.
Results may differ from a plain program's by a relative error of at most 0.0039.
Values may be sent and summed in bfloat16 or wider, within the bound.
No kernel may reach another device: no remote copies, remote signals or barrier semaphores. Data moves between devices by JAX's collectives and lax.ppermute only.
A program may use at most 64 MiB of HBM per device.

v0:
```python
import jax
import jax.numpy as jnp
from jax import lax
from jax.sharding import PartitionSpec as P

PAIR_EPSILON = 1e-05
HIDDEN_EPSILON = 1.0


def layer_norm(values, gain_value, shift_value, along, epsilon):
    center = jnp.mean(values, axis=along, keepdims=True)
    offset = values - center
    spread = jnp.mean(offset * offset, axis=along, keepdims=True)
    return offset * lax.rsqrt(spread + epsilon) * gain_value + shift_value


def project(
    current,
    cell_mask,
    section_index,
    pair_gain,
    pair_shift,
    panel_weight,
    panel_bias,
    gate_weight,
    gate_bias,
):
    normed = layer_norm(
        current, pair_gain[section_index], pair_shift[section_index], 2, PAIR_EPSILON
    ).astype(jnp.bfloat16)
    hidden_width = panel_weight.shape[2] // 4
    features = jnp.einsum(
        "rjc,cf->frj", normed, panel_weight[section_index], preferred_element_type=jnp.float32
    )
    features = features + panel_bias[section_index][:, None, None]
    left_panel = (
        cell_mask
        * jax.nn.sigmoid(features[:hidden_width])
        * features[hidden_width : 2 * hidden_width]
    ).astype(jnp.bfloat16)
    right_panel = (
        cell_mask
        * jax.nn.sigmoid(features[2 * hidden_width : 3 * hidden_width])
        * features[3 * hidden_width :]
    ).astype(jnp.bfloat16)
    gate_value = jax.nn.sigmoid(
        jnp.einsum(
            "rjc,cd->rjd", normed, gate_weight[section_index], preferred_element_type=jnp.float32
        )
        + gate_bias[section_index]
    )
    return (left_panel, right_panel, gate_value)


def local(
    pair_rep,
    residue_mask,
    pair_gain,
    pair_shift,
    panel_weight,
    panel_bias,
    gate_weight,
    gate_bias,
    hidden_gain,
    hidden_shift,
    output_weight,
    output_bias,
):
    row_count = pair_rep.shape[0]
    col_count = pair_rep.shape[1]
    hidden_width = panel_weight.shape[2] // 4
    row_total = lax.axis_size("row")
    col_total = lax.axis_size("ch")
    group = hidden_width // col_total
    if group >= row_total:
        per_slot = group // row_total
        quarters = 1
    else:
        per_slot = 1
        quarters = row_total // group
    slots = row_total // quarters
    sub_rows = row_count // quarters
    blocks = col_count // row_count
    row_index = lax.axis_index("row")
    col_index = lax.axis_index("ch")
    residue_float = residue_mask.astype(jnp.float32)
    row_mask = lax.dynamic_slice_in_dim(residue_float, row_index * row_count, row_count)
    col_mask = lax.dynamic_slice_in_dim(residue_float, col_index * col_count, col_count)
    cell_mask = row_mask[:, None] * col_mask[None, :]
    current = pair_rep
    for section_index in range(2):
        left_panel, right_panel, gate_value = project(
            current,
            cell_mask,
            section_index,
            pair_gain,
            pair_shift,
            panel_weight,
            panel_bias,
            gate_weight,
            gate_bias,
        )
        if section_index == 0:
            send_left = left_panel.reshape(
                col_total, slots, per_slot, quarters, sub_rows, col_count
            )
            send_left = jnp.transpose(send_left, (0, 1, 3, 2, 4, 5)).reshape(
                col_total, row_total, per_slot, sub_rows, col_count
            )
        else:
            send_left = left_panel.reshape(
                col_total, slots, per_slot, row_count, blocks, quarters, sub_rows
            )
            send_left = jnp.transpose(send_left, (0, 1, 5, 2, 3, 4, 6)).reshape(
                col_total, row_total, per_slot, row_count, blocks * sub_rows
            )
        send_right = right_panel.reshape(col_total, slots, 1, per_slot, row_count, col_count)
        send_right = jnp.broadcast_to(
            send_right, (col_total, slots, quarters, per_slot, row_count, col_count)
        ).reshape(col_total, row_total, per_slot, row_count, col_count)
        got_left, got_right = (
            lax.all_to_all(
                lax.all_to_all(send_left, "ch", split_axis=0, concat_axis=4, tiled=True),
                "row",
                split_axis=1,
                concat_axis=3,
                tiled=True,
            ),
            lax.all_to_all(
                lax.all_to_all(send_right, "ch", split_axis=0, concat_axis=4, tiled=True),
                "row",
                split_axis=1,
                concat_axis=3,
                tiled=True,
            ),
        )
        got_left = got_left[0, 0]
        got_right = got_right[0, 0]
        if section_index == 0:
            products = jnp.einsum(
                "hik,hjk->hij", got_left, got_right, preferred_element_type=jnp.float32
            )
        else:
            products = jnp.einsum(
                "hki,hkj->hij", got_left, got_right, preferred_element_type=jnp.float32
            )
        returned = products.reshape(per_slot, row_total, sub_rows, col_total, col_count)
        gathered = lax.all_to_all(
            lax.all_to_all(returned, "row", split_axis=1, concat_axis=0, tiled=True),
            "ch",
            split_axis=3,
            concat_axis=0,
            tiled=True,
        )
        gathered = gathered.reshape(col_total, slots, quarters, per_slot, sub_rows, col_count)
        gathered = jnp.transpose(gathered, (0, 1, 3, 2, 4, 5)).reshape(
            hidden_width, row_count, col_count
        )
        normed = layer_norm(
            gathered,
            hidden_gain[section_index][:, None, None],
            hidden_shift[section_index][:, None, None],
            0,
            HIDDEN_EPSILON,
        ).astype(jnp.bfloat16)
        projected = jnp.einsum(
            "hrj,hc->rjc", normed, output_weight[section_index], preferred_element_type=jnp.float32
        )
        current = current + gate_value * (projected + output_bias[section_index])
    return current


def solution(mesh):
    return jax.shard_map(
        local,
        mesh=mesh,
        in_specs=(P("row", "ch", None), P(), P(), P(), P(), P(), P(), P(), P(), P(), P(), P()),
        out_specs=P("row", "ch", None),
        check_vma=False,
    )
```

profile of v0, /device:TPU:1, one launch (start us, length us, event | category | flops | bytes accessed | tf_op | source)
XLA Modules:
  0.0 237.8 jit_solution(15132575258035576822)
XLA Ops:
  0.0 0.7 convert_element_type.34
  0.8 1.6 reduce_sum.72
  2.4 1.9 multiply_reduce_fusion.3
  4.3 0.8 slice_bitcast_fusion.3
  5.1 0.8 fusion.46
  5.9 0.8 slice_bitcast_fusion.1
  6.7 2.1 add_bitcast_fusion.1
  8.8 0.6 fusion.22
  9.4 1.2 copy.82
  10.6 3.5 %all-to-all-start = ((bf16[2,16,4,16,128]{4,3,2,1,0:T(8,128)(2,1)}), bf16[2,16,4,16,128]{4,3,2,1,0:T(8,128)(2,1)S(1)}, u32[]{:S(2)}, u32[]{:S(2)}) async-start(bf16[2,16,4,16,128]{4,3,2,1,0:T(8,128)(2,1)} %bitcast.9), calls=%async_computation | async-start | bytes 1048576 | tf_op jit(solution)/shard_map/all_to_all | solution.py:123
  14.1 1.2 copy.86
  15.3 7.1 %all-to-all-done = bf16[2,16,4,16,128]{4,3,2,1,0:T(8,128)(2,1)S(1)} async-done(((bf16[2,16,4,16,128]{4,3,2,1,0:T(8,128)(2,1)}), bf16[2,16,4,16,128]{4,3,2,1,0:T(8,128)(2,1)S(1)}, u32[]{:S(2)}, u32[]{:S(2)}) %all-to-all-start) | async-done | bytes 524320 | tf_op jit(solution)/shard_map/all_to_all | solution.py:123
  22.4 3.5 %all-to-all-start.2 = ((bf16[2,16,4,16,128]{4,3,2,1,0:T(8,128)(2,1)}), bf16[2,16,4,16,128]{4,3,2,1,0:T(8,128)(2,1)S(1)}, u32[]{:S(2)}, u32[]{:S(2)}) async-start(bf16[2,16,4,16,128]{4,3,2,1,0:T(8,128)(2,1)} %bitcast.16), calls=%async_computation.2 | async-start | bytes 1048576 | tf_op jit(solution)/shard_map/all_to_all | solution.py:130
  25.9 0.9 bitcast_bitcast_fusion.3
  26.7 5.9 %all-to-all-done.2 = bf16[2,16,4,16,128]{4,3,2,1,0:T(8,128)(2,1)S(1)} async-done(((bf16[2,16,4,16,128]{4,3,2,1,0:T(8,128)(2,1)}), bf16[2,16,4,16,128]{4,3,2,1,0:T(8,128)(2,1)S(1)}, u32[]{:S(2)}, u32[]{:S(2)}) %all-to-all-start.2) | async-done | bytes 524320 | tf_op jit(solution)/shard_map/all_to_all | solution.py:130
  32.7 7.9 %all-to-all-start.1 = ((bf16[1,16,4,16,256]{4,3,2,0,1:T(8,128)(2,1)}), bf16[1,16,4,16,256]{4,3,2,0,1:T(8,128)(2,1)S(1)}, u32[]{:S(2)}, u32[]{:S(2)}) async-start(bf16[1,16,4,16,256]{4,3,2,0,1:T(8,128)(2,1)} %bitcast_bitcast_fusion.3), calls=%async_computation.1 | async-start | bytes 1048576 | tf_op jit(solution)/shard_map/all_to_all | solution.py:122
  40.5 0.9 bitcast_bitcast_fusion.2
  41.4 13.2 %all-to-all-done.1 = bf16[1,16,4,16,256]{4,3,2,0,1:T(8,128)(2,1)S(1)} async-done(((bf16[1,16,4,16,256]{4,3,2,0,1:T(8,128)(2,1)}), bf16[1,16,4,16,256]{4,3,2,0,1:T(8,128)(2,1)S(1)}, u32[]{:S(2)}, u32[]{:S(2)}) %all-to-all-start.1) | async-done | bytes 524320 | tf_op jit(solution)/shard_map/all_to_all | solution.py:122
  54.5 4.4 %all-to-all-start.3 = ((bf16[1,16,4,16,256]{4,3,2,0,1:T(8,128)(2,1)}), bf16[1,16,4,16,256]{4,3,2,0,1:T(8,128)(2,1)S(1)}, u32[]{:S(2)}, u32[]{:S(2)}) async-start(bf16[1,16,4,16,256]{4,3,2,0,1:T(8,128)(2,1)} %bitcast_bitcast_fusion.2), calls=%async_computation.3 | async-start | bytes 1048576 | tf_op jit(solution)/shard_map/all_to_all | solution.py:129
  59.0 14.0 %all-to-all-done.3 = bf16[1,16,4,16,256]{4,3,2,0,1:T(8,128)(2,1)S(1)} async-done(((bf16[1,16,4,16,256]{4,3,2,0,1:T(8,128)(2,1)}), bf16[1,16,4,16,256]{4,3,2,0,1:T(8,128)(2,1)S(1)}, u32[]{:S(2)}, u32[]{:S(2)}) %all-to-all-start.3) | async-done | bytes 524320 | tf_op jit(solution)/shard_map/all_to_all | solution.py:129
  73.4 0.5 reshape.111
  74.1 29.6 %all_to_all.198 = f32[4,16,16,2,128]{4,2,3,0,1:T(8,128)S(1)} all-to-all(f32[4,16,16,2,128]{4,2,3,0,1:T(8,128)S(1)} %copy.90), channel_id=1, replica_groups=mesh['row'=16,'ch'=2] {'row'}, dimensions={1} | all-to-all | bytes 2097152 | tf_op jit(solution)/shard_map/all_to_all | solution.py:149
  103.7 1.1 copy.91
  104.7 3.6 %all-to-all-start.5 = ((f32[64,1,16,2,128]{4,2,1,0,3:T(8,128)}), f32[64,1,16,2,128]{4,2,1,0,3:T(8,128)S(1)}, u32[]{:S(2)}, u32[]{:S(2)}) async-start(f32[64,1,16,2,128]{4,2,1,0,3:T(8,128)} %copy.91), calls=%async_computation.5 | async-start | bytes 2097152 | tf_op jit(solution)/shard_map/all_to_all | solution.py:148
  108.9 2.0 fusion.11
  110.9 11.5 %all-to-all-done.5 = f32[64,1,16,2,128]{4,2,1,0,3:T(8,128)S(1)} async-done(((f32[64,1,16,2,128]{4,2,1,0,3:T(8,128)}), f32[64,1,16,2,128]{4,2,1,0,3:T(8,128)S(1)}, u32[]{:S(2)}, u32[]{:S(2)}) %all-to-all-start.5) | async-done | bytes 1048608 | tf_op jit(solution)/shard_map/all_to_all | solution.py:148
  123.1 0.5 copy-done.1
  124.2 0.8 add_bitcast_fusion
  125.0 0.6 fusion.12
  125.7 1.2 copy.102
  126.8 3.5 %all-to-all-start.8 = ((bf16[2,16,4,16,128]{4,3,2,1,0:T(8,128)(2,1)}), bf16[2,16,4,16,128]{4,3,2,1,0:T(8,128)(2,1)S(1)}, u32[]{:S(2)}, u32[]{:S(2)}) async-start(bf16[2,16,4,16,128]{4,3,2,1,0:T(8,128)(2,1)} %bitcast.49), calls=%async_computation.8 | async-start | bytes 1048576 | tf_op jit(solution)/shard_map/all_to_all | solution.py:130
  130.3 1.2 copy.98
  131.5 6.5 %all-to-all-done.8 = bf16[2,16,4,16,128]{4,3,2,1,0:T(8,128)(2,1)S(1)} async-done(((bf16[2,16,4,16,128]{4,3,2,1,0:T(8,128)(2,1)}), bf16[2,16,4,16,128]{4,3,2,1,0:T(8,128)(2,1)S(1)}, u32[]{:S(2)}, u32[]{:S(2)}) %all-to-all-start.8) | async-done | bytes 524320 | tf_op jit(solution)/shard_map/all_to_all | solution.py:130
  138.0 3.5 %all-to-all-start.6 = ((bf16[2,16,4,16,128]{4,3,2,1,0:T(8,128)(2,1)}), bf16[2,16,4,16,128]{4,3,2,1,0:T(8,128)(2,1)S(1)}, u32[]{:S(2)}, u32[]{:S(2)}) async-start(bf16[2,16,4,16,128]{4,3,2,1,0:T(8,128)(2,1)} %bitcast.42), calls=%async_computation.6 | async-start | bytes 1048576 | tf_op jit(solution)/shard_map/all_to_all | solution.py:123
  141.5 0.9 bitcast_bitcast_fusion
  142.3 5.9 %all-to-all-done.6 = bf16[2,16,4,16,128]{4,3,2,1,0:T(8,128)(2,1)S(1)} async-done(((bf16[2,16,4,16,128]{4,3,2,1,0:T(8,128)(2,1)}), bf16[2,16,4,16,128]{4,3,2,1,0:T(8,128)(2,1)S(1)}, u32[]{:S(2)}, u32[]{:S(2)}) %all-to-all-start.6) | async-done | bytes 524320 | tf_op jit(solution)/shard_map/all_to_all | solution.py:123
  148.3 5.5 %all-to-all-start.9 = ((bf16[1,16,4,16,256]{4,3,2,0,1:T(8,128)(2,1)}), bf16[1,16,4,16,256]{4,3,2,0,1:T(8,128)(2,1)S(1)}, u32[]{:S(2)}, u32[]{:S(2)}) async-start(bf16[1,16,4,16,256]{4,3,2,0,1:T(8,128)(2,1)} %bitcast_bitcast_fusion), calls=%async_computation.9 | async-start | bytes 1048576 | tf_op jit(solution)/shard_map/all_to_all | solution.py:129
  153.8 0.9 bitcast_bitcast_fusion.1
  154.6 13.2 %all-to-all-done.9 = bf16[1,16,4,16,256]{4,3,2,0,1:T(8,128)(2,1)S(1)} async-done(((bf16[1,16,4,16,256]{4,3,2,0,1:T(8,128)(2,1)}), bf16[1,16,4,16,256]{4,3,2,0,1:T(8,128)(2,1)S(1)}, u32[]{:S(2)}, u32[]{:S(2)}) %all-to-all-start.9) | async-done | bytes 524320 | tf_op jit(solution)/shard_map/all_to_all | solution.py:129
  167.8 4.4 %all-to-all-start.7 = ((bf16[1,16,4,16,256]{4,3,2,0,1:T(8,128)(2,1)}), bf16[1,16,4,16,256]{4,3,2,0,1:T(8,128)(2,1)S(1)}, u32[]{:S(2)}, u32[]{:S(2)}) async-start(bf16[1,16,4,16,256]{4,3,2,0,1:T(8,128)(2,1)} %bitcast_bitcast_fusion.1), calls=%async_computation.7 | async-start | bytes 1048576 | tf_op jit(solution)/shard_map/all_to_all | solution.py:122
  172.3 14.0 %all-to-all-done.7 = bf16[1,16,4,16,256]{4,3,2,0,1:T(8,128)(2,1)S(1)} async-done(((bf16[1,16,4,16,256]{4,3,2,0,1:T(8,128)(2,1)}), bf16[1,16,4,16,256]{4,3,2,0,1:T(8,128)(2,1)S(1)}, u32[]{:S(2)}, u32[]{:S(2)}) %all-to-all-start.7) | async-done | bytes 524320 | tf_op jit(solution)/shard_map/all_to_all | solution.py:122
  186.6 0.5 reshape.112
  187.3 29.5 %all_to_all.199 = f32[4,16,16,2,128]{4,2,3,0,1:T(8,128)S(1)} all-to-all(f32[4,16,16,2,128]{4,2,3,0,1:T(8,128)S(1)} %copy.107), channel_id=1, replica_groups=mesh['row'=16,'ch'=2] {'row'}, dimensions={1} | all-to-all | bytes 2097152 | tf_op jit(solution)/shard_map/all_to_all | solution.py:149
  216.7 1.1 copy.108
  217.8 3.6 %all-to-all-start.11 = ((f32[64,1,16,2,128]{4,2,1,0,3:T(8,128)}), f32[64,1,16,2,128]{4,2,1,0,3:T(8,128)S(1)}, u32[]{:S(2)}, u32[]{:S(2)}) async-start(f32[64,1,16,2,128]{4,2,1,0,3:T(8,128)} %copy.108), calls=%async_computation.11 | async-start | bytes 2097152 | tf_op jit(solution)/shard_map/all_to_all | solution.py:148
  221.5 0.5 fusion.7
  222.1 13.4 %all-to-all-done.11 = f32[64,1,16,2,128]{4,2,1,0,3:T(8,128)S(1)} async-done(((f32[64,1,16,2,128]{4,2,1,0,3:T(8,128)}), f32[64,1,16,2,128]{4,2,1,0,3:T(8,128)S(1)}, u32[]{:S(2)}, u32[]{:S(2)}) %all-to-all-start.11) | async-done | bytes 1048608 | tf_op jit(solution)/shard_map/all_to_all | solution.py:148
  236.5 1.3 copy.111
  (52 shorter events, 4.1 us)
Async XLA Ops:
  10.6 11.7 %all-to-all-start = ((bf16[2,16,4,16,128]{4,3,2,1,0:T(8,128)(2,1)}), bf16[2,16,4,16,128]{4,3,2,1,0:T(8,128)(2,1)S(1)}, u32[]{:S(2)}, u32[]{:S(2)}) async-start(bf16[2,16,4,16,128]{4,3,2,1,0:T(8,128)(2,1)} %bitcast.9), calls=%async_computation | async-start | bytes 1048576 | tf_op jit(solution)/shard_map/all_to_all | solution.py:123
  22.4 10.3 %all-to-all-start.2 = ((bf16[2,16,4,16,128]{4,3,2,1,0:T(8,128)(2,1)}), bf16[2,16,4,16,128]{4,3,2,1,0:T(8,128)(2,1)S(1)}, u32[]{:S(2)}, u32[]{:S(2)}) async-start(bf16[2,16,4,16,128]{4,3,2,1,0:T(8,128)(2,1)} %bitcast.16), calls=%async_computation.2 | async-start | bytes 1048576 | tf_op jit(solution)/shard_map/all_to_all | solution.py:130
  32.7 21.9 %all-to-all-start.1 = ((bf16[1,16,4,16,256]{4,3,2,0,1:T(8,128)(2,1)}), bf16[1,16,4,16,256]{4,3,2,0,1:T(8,128)(2,1)S(1)}, u32[]{:S(2)}, u32[]{:S(2)}) async-start(bf16[1,16,4,16,256]{4,3,2,0,1:T(8,128)(2,1)} %bitcast_bitcast_fusion.3), calls=%async_computation.1 | async-start | bytes 1048576 | tf_op jit(solution)/shard_map/all_to_all | solution.py:122
  54.5 18.4 %all-to-all-start.3 = ((bf16[1,16,4,16,256]{4,3,2,0,1:T(8,128)(2,1)}), bf16[1,16,4,16,256]{4,3,2,0,1:T(8,128)(2,1)S(1)}, u32[]{:S(2)}, u32[]{:S(2)}) async-start(bf16[1,16,4,16,256]{4,3,2,0,1:T(8,128)(2,1)} %bitcast_bitcast_fusion.2), calls=%async_computation.3 | async-start | bytes 1048576 | tf_op jit(solution)/shard_map/all_to_all | solution.py:129
  73.9 34.4 %copy-start.5 = (f32[2,128]{1,0:T(2,128)S(1)}, f32[2,128]{1,0:T(2,128)}, u32[]{:S(2)}) copy-start(f32[2,128]{1,0:T(2,128)} %param.21) | copy-start | bytes 3076
  73.9 34.4 %copy-start.6 = (f32[2,128]{1,0:T(2,128)S(1)}, f32[2,128]{1,0:T(2,128)}, u32[]{:S(2)}) copy-start(f32[2,128]{1,0:T(2,128)} %param.20) | copy-start | bytes 3076
  73.9 34.4 %copy-start = (f32[16,128,128]{2,1,0:T(8,128)S(1)}, f32[16,128,128]{2,1,0:T(8,128)}, u32[]{:S(2)}) copy-start(f32[16,128,128]{2,1,0:T(8,128)} %param.12) | copy-start | bytes 3145732
  74.1 34.8 %copy-start.4 = (f32[2,128]{1,0:T(2,128)S(1)}, f32[2,128]{1,0:T(2,128)}, u32[]{:S(2)}) copy-start(f32[2,128]{1,0:T(2,128)} %param.23) | copy-start | bytes 3076
  74.1 34.8 %copy-start.7 = (bf16[2,128,128]{2,1,0:T(8,128)(2,1)S(1)}, bf16[2,128,128]{2,1,0:T(8,128)(2,1)}, u32[]{:S(2)}) copy-start(bf16[2,128,128]{2,1,0:T(8,128)(2,1)} %param.18) | copy-start | bytes 196612
  104.7 17.7 %all-to-all-start.5 = ((f32[64,1,16,2,128]{4,2,1,0,3:T(8,128)}), f32[64,1,16,2,128]{4,2,1,0,3:T(8,128)S(1)}, u32[]{:S(2)}, u32[]{:S(2)}) async-start(f32[64,1,16,2,128]{4,2,1,0,3:T(8,128)} %copy.91), calls=%async_computation.5 | async-start | bytes 2097152 | tf_op jit(solution)/shard_map/all_to_all | solution.py:148
  108.9 14.2 %copy-start.3 = (bf16[2,128,128]{2,1,0:T(8,128)(2,1)S(1)}, bf16[2,128,128]{2,1,0:T(8,128)(2,1)}, u32[]{:S(2)}) copy-start(bf16[2,128,128]{2,1,0:T(8,128)(2,1)} %param.22) | copy-start | bytes 196612
  110.9 13.3 %copy-start.2 = (bf16[2,128,512]{2,1,0:T(8,128)(2,1)S(1)}, bf16[2,128,512]{2,1,0:T(8,128)(2,1)}, u32[]{:S(2)}) copy-start(bf16[2,128,512]{2,1,0:T(8,128)(2,1)} %param.16) | copy-start | bytes 786436
  122.5 1.2 copy-start.1
  126.8 11.2 %all-to-all-start.8 = ((bf16[2,16,4,16,128]{4,3,2,1,0:T(8,128)(2,1)}), bf16[2,16,4,16,128]{4,3,2,1,0:T(8,128)(2,1)S(1)}, u32[]{:S(2)}, u32[]{:S(2)}) async-start(bf16[2,16,4,16,128]{4,3,2,1,0:T(8,128)(2,1)} %bitcast.49), calls=%async_computation.8 | async-start | bytes 1048576 | tf_op jit(solution)/shard_map/all_to_all | solution.py:130
  138.0 10.3 %all-to-all-start.6 = ((bf16[2,16,4,16,128]{4,3,2,1,0:T(8,128)(2,1)}), bf16[2,16,4,16,128]{4,3,2,1,0:T(8,128)(2,1)S(1)}, u32[]{:S(2)}, u32[]{:S(2)}) async-start(bf16[2,16,4,16,128]{4,3,2,1,0:T(8,128)(2,1)} %bitcast.42), calls=%async_computation.6 | async-start | bytes 1048576 | tf_op jit(solution)/shard_map/all_to_all | solution.py:123
  148.3 19.5 %all-to-all-start.9 = ((bf16[1,16,4,16,256]{4,3,2,0,1:T(8,128)(2,1)}), bf16[1,16,4,16,256]{4,3,2,0,1:T(8,128)(2,1)S(1)}, u32[]{:S(2)}, u32[]{:S(2)}) async-start(bf16[1,16,4,16,256]{4,3,2,0,1:T(8,128)(2,1)} %bitcast_bitcast_fusion), calls=%async_computation.9 | async-start | bytes 1048576 | tf_op jit(solution)/shard_map/all_to_all | solution.py:129
  167.8 18.4 %all-to-all-start.7 = ((bf16[1,16,4,16,256]{4,3,2,0,1:T(8,128)(2,1)}), bf16[1,16,4,16,256]{4,3,2,0,1:T(8,128)(2,1)S(1)}, u32[]{:S(2)}, u32[]{:S(2)}) async-start(bf16[1,16,4,16,256]{4,3,2,0,1:T(8,128)(2,1)} %bitcast_bitcast_fusion.1), calls=%async_computation.7 | async-start | bytes 1048576 | tf_op jit(solution)/shard_map/all_to_all | solution.py:122
  187.2 34.4 %copy-start.8 = (bf16[2,128,128]{2,1,0:T(8,128)(2,1)S(1)}, bf16[2,128,128]{2,1,0:T(8,128)(2,1)}, u32[]{:S(2)}) copy-start(bf16[2,128,128]{2,1,0:T(8,128)(2,1)} %param.18) | copy-start | bytes 196612
  217.8 17.7 %all-to-all-start.11 = ((f32[64,1,16,2,128]{4,2,1,0,3:T(8,128)}), f32[64,1,16,2,128]{4,2,1,0,3:T(8,128)S(1)}, u32[]{:S(2)}, u32[]{:S(2)}) async-start(f32[64,1,16,2,128]{4,2,1,0,3:T(8,128)} %copy.108), calls=%async_computation.11 | async-start | bytes 2097152 | tf_op jit(solution)/shard_map/all_to_all | solution.py:148
where the time goes:
time: 240 us; the launch traced here: 238 us
  waiting for transfers between devices  105 us (44%)
  blocking collectives  59.1 us (25%)
  starting transfers between devices  43.3 us (18%)
  local copies, waits for them, and re-layouts  16.7 us (7%)
  matrix products  6.9 us (3%)
  other arithmetic  6.83 us (3%)
    all_to_all x2, blocking collectives, local(): lax.all_to_all(returned, 'row', split_axis=1, concat_axis=0, tiled=True)  59.1 us
    all_to_all x2, waiting for transfers between devices, local(): lax.all_to_all(lax.all_to_all(send_right, 'ch', split_axis=0, concat_axis...  27.2 us
    all_to_all x2, waiting for transfers between devices, local(): lax.all_to_all(lax.all_to_all(send_left, 'ch', split_axis=0, concat_axis=...  27.1 us
    all_to_all x2, waiting for transfers between devices, local(): lax.all_to_all(lax.all_to_all(returned, 'row', split_axis=1, concat_axis=...  25 us
    all_to_all x2, waiting for transfers between devices, local(): lax.all_to_all(send_left, 'ch', split_axis=0, concat_axis=4, tiled=True)  13 us
    all_to_all x2, waiting for transfers between devices, local(): lax.all_to_all(send_right, 'ch', split_axis=0, concat_axis=4, tiled=True)  12.4 us
    all_to_all x2, starting transfers between devices, local(): lax.all_to_all(lax.all_to_all(send_left, 'ch', split_axis=0, concat_axis=...  12.3 us
    all_to_all x2, starting transfers between devices, local(): lax.all_to_all(lax.all_to_all(send_right, 'ch', split_axis=0, concat_axis...  9.91 us
  transfers between devices with their start and end apart: 10, of which 10 were waited for; matrix products, arithmetic and copies ran while one was open for 4% of the time, Pallas kernels for 0%

commit v1 on v0

--- a/solution.py
+++ b/solution.py
@@ -50,6 +50,29 @@
         + gate_bias[section_index]
     )
     return (left_panel, right_panel, gate_value)
+
+
+def finish(
+    gathered,
+    current,
+    gate_value,
+    section_index,
+    hidden_gain,
+    hidden_shift,
+    output_weight,
+    output_bias,
+):
+    normed = layer_norm(
+        gathered,
+        hidden_gain[section_index][:, None, None],
+        hidden_shift[section_index][:, None, None],
+        0,
+        HIDDEN_EPSILON,
+    ).astype(jnp.bfloat16)
+    projected = jnp.einsum(
+        "hrj,hc->rjc", normed, output_weight[section_index], preferred_element_type=jnp.float32
+    )
+    return current + gate_value * (projected + output_bias[section_index])
 
 
 def local(
@@ -88,6 +111,8 @@
     col_mask = lax.dynamic_slice_in_dim(residue_float, col_index * col_count, col_count)
     cell_mask = row_mask[:, None] * col_mask[None, :]
     current = pair_rep
+    devices = row_total * col_total
+    direct = hidden_width % devices == 0
     for section_index in range(2):
         left_panel, right_panel, gate_value = project(
             current,
@@ -100,6 +125,43 @@
             gate_weight,
             gate_bias,
         )
+        if direct:
+            own = hidden_width // devices
+            send = jnp.concatenate(
+                [
+                    left_panel.reshape(devices, own, row_count, col_count),
+                    right_panel.reshape(devices, own, row_count, col_count),
+                ],
+                axis=1,
+            )
+            got = lax.all_to_all(send, ("row", "ch"), split_axis=0, concat_axis=0, tiled=True)
+            got = got.reshape(row_total, col_total, 2 * own, row_count, col_count)
+            got = jnp.transpose(got, (2, 0, 3, 1, 4)).reshape(
+                2 * own, row_total * row_count, col_total * col_count
+            )
+            pattern = "hik,hjk->hij" if section_index == 0 else "hki,hkj->hij"
+            products = jnp.einsum(
+                pattern, got[:own], got[own:], preferred_element_type=jnp.float32
+            ).astype(jnp.bfloat16)
+            returned = products.reshape(own, row_total, row_count, col_total, col_count)
+            returned = jnp.transpose(returned, (1, 3, 0, 2, 4)).reshape(
+                devices, own, row_count, col_count
+            )
+            gathered = lax.all_to_all(
+                returned, ("row", "ch"), split_axis=0, concat_axis=0, tiled=True
+            )
+            gathered = gathered.reshape(hidden_width, row_count, col_count).astype(jnp.float32)
+            current = finish(
+                gathered,
+                current,
+                gate_value,
+                section_index,
+                hidden_gain,
+                hidden_shift,
+                output_weight,
+                output_bias,
+            )
+            continue
         if section_index == 0:
             send_left = left_panel.reshape(
                 col_total, slots, per_slot, quarters, sub_rows, col_count
@@ -156,17 +218,16 @@
         gathered = jnp.transpose(gathered, (0, 1, 3, 2, 4, 5)).reshape(
             hidden_width, row_count, col_count
         )
-        normed = layer_norm(
+        current = finish(
             gathered,
-            hidden_gain[section_index][:, None, None],
-            hidden_shift[section_index][:, None, None],
-            0,
-            HIDDEN_EPSILON,
-        ).astype(jnp.bfloat16)
-        projected = jnp.einsum(
-            "hrj,hc->rjc", normed, output_weight[section_index], preferred_element_type=jnp.float32
-        )
-        current = current + gate_value * (projected + output_bias[section_index])
+            current,
+            gate_value,
+            section_index,
+            hidden_gain,
+            hidden_shift,
+            output_weight,
+            output_bias,
+        )
     return current
 
 

time: 240 us -> 128 us (0.53)
  waiting for transfers between devices: 105 us -> 28.3 us
  starting transfers between devices: 43.3 us -> 7.51 us
  blocking collectives: 59.1 us -> 61.6 us
    all_to_all x10 -> x2, waiting for transfers between devices: 105 us -> 28.3 us  [local(): lax.all_to_all(returned, ('row', 'ch'), split_axis=0, concat_axis=0, tile...]
    all_to_all x10 -> x2, starting transfers between devices: 43.3 us -> 7.51 us  [local(): lax.all_to_all(returned, ('row', 'ch'), split_axis=0, concat_axis=0, tile...]
    all_to_all x10 -> x0, local copies, waits for them, and re-layouts: 5.7 us -> none  [the longest x2 2.11 us: local(): lax.all_to_all(returned, 'row', split_axis=1, concat_axis=0, tiled=True)]
    reshape x4 -> x6, local copies, waits for them, and re-layouts: 1.26 us -> 5.33 us  [the longest x2 3.24 us: local(): got = got.reshape(row_total, col_total, 2 * own, row_count, col_count)]
    slice x1 -> x7, local copies, waits for them, and re-layouts: 0.02 us -> 2.88 us  [the longest x4 2.19 us: local(): got[own:]]
    all_to_all x2, blocking collectives: 59.1 us -> 61.6 us  [local(): lax.all_to_all(send, ('row', 'ch'), split_axis=0, concat_axis=0, tiled=True)]
  transfers between devices with their start and end apart: 10 -> 2, of which waited for: 10 -> 2; matrix products, arithmetic and copies ran while one was open for 4% -> 3% of each run, Pallas kernels for 0% -> 0%
where the time goes in v1:
time: 128 us; the launch traced here: 127 us
  blocking collectives  61.6 us (48%)
  waiting for transfers between devices  28.3 us (22%)
  local copies, waits for them, and re-layouts  14.4 us (11%)
  matrix products  8.13 us (6%)
  starting transfers between devices  7.51 us (6%)
  other arithmetic  7.1 us (6%)
    all_to_all x2, blocking collectives, local(): lax.all_to_all(send, ('row', 'ch'), split_axis=0, concat_axis=0, tiled=True)  61.6 us
    all_to_all x2, waiting for transfers between devices, local(): lax.all_to_all(returned, ('row', 'ch'), split_axis=0, concat_axis=0, tile...  28.3 us
    all_to_all x2, starting transfers between devices, local(): lax.all_to_all(returned, ('row', 'ch'), split_axis=0, concat_axis=0, tile...  7.51 us
    reshape x2, local copies, waits for them, and re-layouts, local(): got = got.reshape(row_total, col_total, 2 * own, row_count, col_count)  3.24 us
    dot_general x2, matrix products, project(): jnp.einsum('rjc,cf->frj', normed, panel_weight[section_index], preferred_...  2.99 us
  transfers between devices with their start and end apart: 2, of which 2 were waited for; matrix products, arithmetic and copies ran while one was open for 3% of the time, Pallas kernels for 0%

profile of v1, /device:TPU:1, one launch (start us, length us, event | category | flops | bytes accessed | tf_op | source)
XLA Modules:
  0.0 127.5 jit_solution(3480858212297803509)
XLA Ops:
  0.0 0.7 convert_element_type.52
  0.8 1.6 %reduce_sum.72 = f32[16,128]{1,0:T(8,128)S(1)} reduce(f32[16,128,128]{2,1,0:T(8,128)} %param.12, f32[]{:T(128)} %constant.12.clone.1), dimensions={2}, to_apply=%region_0.0 | reduce | flops 260096 | bytes 1056772 | tf_op jit(solution)/shard_map/reduce_sum | solution.py:11
  2.4 1.9 %multiply_reduce_fusion.1 = f32[16,128]{1,0:T(8,128)S(1)} fusion(f32[16,128,128]{2,1,0:T(8,128)} %param.12, f32[16,128]{1,0:T(8,128)S(1)} %broadcast_multiply_fusion.4), kind=kLoop, calls=%fused_computation.71 | loop fusion | flops 784384 | bytes 1064960 | tf_op jit(solution)/shard_map/reduce_sum | solution.py:13
  4.3 0.8 slice_bitcast_fusion.3
  5.1 0.8 fusion.60
  5.9 0.8 slice_bitcast_fusion.1
  6.7 2.1 %add_bitcast_fusion.1 = f32[512,16,128]{0,2,1:T(8,128)S(1)} fusion(f32[512]{0:T(512)S(1)} %bitcast.85, bf16[2,128,512]{2,1,0:T(8,128)(2,1)} %param.16, f32[16,128,128]{2,1,0:T(8,128)} %param.12, f32[128]{0:T(128)S(1)} %get-tuple-element.29, f32[128]{0:T(128)S(1)} %get-tuple-element.22, f32[16,128]{1,0:T(8,128)S(1)} %add_rsqrt_fusion.3, ...), kind=kOutput, calls=%fused_computation.1 | convolution fusion | flops 270794752 | bytes 5393408 | tf_op jit(solution)/shard_map/rjc,cf->frj/dot_general | solution.py:32
  8.8 0.6 fusion.39
  9.4 0.4 copy.26
  9.9 0.4 copy.25
  10.4 33.0 %all_to_all.20 = bf16[32,8,16,128]{3,2,1,0:T(8,128)(2,1)S(1)} all-to-all(bf16[32,8,16,128]{3,2,1,0:T(8,128)(2,1)S(1)} %pad_maximum_fusion), channel_id=1, replica_groups=mesh['row'=16,'ch'=2] {'row','ch'}, dimensions={0} | all-to-all | bytes 2097152 | tf_op jit(solution)/shard_map/all_to_all | solution.py:137
  43.3 1.6 %copy.59 = bf16[16,2,8,16,128]{4,1,3,0,2:T(2,128)(2,1)S(1)} copy(bf16[16,2,8,16,128]{4,3,2,1,0:T(8,128)(2,1)S(1)} %bitcast.76) | data formatting | bytes 2097152 | tf_op jit(solution)/shard_map/reshape | solution.py:138
  45.0 0.8 fusion.59
  45.8 0.3 slice.119
  46.1 0.3 slice.121
  46.5 0.3 convolution_convert_fusion.1
  46.8 0.1 reshape.140
  47.0 0.9 copy.28
  47.9 3.8 %all-to-all-start.1 = ((bf16[32,4,16,128]{3,2,1,0:T(8,128)(2,1)}), bf16[32,4,16,128]{3,2,1,0:T(8,128)(2,1)S(1)}, u32[]{:S(2)}, u32[]{:S(2)}) async-start(bf16[32,4,16,128]{3,2,1,0:T(8,128)(2,1)} %bitcast.14), calls=%async_computation.1 | async-start | bytes 1048576 | tf_op jit(solution)/shard_map/all_to_all | solution.py:150
  51.6 0.3 copy.31
  52.3 2.0 %fusion.11 = f32[16,128,128]{1,2,0:T(8,128)} fusion(f32[128]{0:T(128)S(1)} %get-tuple-element.26, bf16[2,128,128]{2,1,0:T(8,128)(2,1)S(1)} %copy-done.6, f32[16,128,128]{2,1,0:T(8,128)S(1)} %copy-done, f32[128]{0:T(128)S(1)} %get-tuple-element.29, f32[128]{0:T(128)S(1)} %get-tuple-element.22, f32[16,128]{1,0:T(8,128)S(1)} %add_rsqrt_fusion.3, ...), kind=kOutput, calls=%fused_computation.17 | convolution fusion | flops 69468160 | bytes 2147840 | tf_op jit(solution)/shard_map/rjc,cd->rjd/dot_general | solution.py:47
  54.3 13.2 %all-to-all-done.1 = bf16[32,4,16,128]{3,2,1,0:T(8,128)(2,1)S(1)} async-done(((bf16[32,4,16,128]{3,2,1,0:T(8,128)(2,1)}), bf16[32,4,16,128]{3,2,1,0:T(8,128)(2,1)S(1)}, u32[]{:S(2)}, u32[]{:S(2)}) %all-to-all-start.1) | async-done | bytes 524320 | tf_op jit(solution)/shard_map/all_to_all | solution.py:150
  67.5 0.1 convert_reduce_fusion.1
  67.6 0.2 fusion.20
  67.8 0.3 fusion.23
  68.2 1.6 %fusion.61 = (f32[16,128]{1,0:T(8,128)S(1)}, f32[16,128,128]{1,2,0:T(8,128)S(1)}) fusion(f32[16,128,128]{1,2,0:T(8,128)S(1)} %copy.31, f32[16,128,128]{1,2,0:T(8,128)} %fusion.11, f32[128]{0:T(128)S(1)} %get-tuple-element.20, bf16[128,16,128]{2,1,0:T(8,128)(2,1)S(1)} %bitcast.78, bf16[2,128,128]{2,1,0:T(8,128)(2,1)S(1)} %copy-done.2), kind=kOutput, calls=%fused_computation.110 | convolution fusion | flops 68155392 | bytes 3711488 | tf_op jit(solution)/shard_map/hrj,hc->rjc/dot_general | solution.py:72
  69.8 0.1 multiply_reduce_fusion
  70.0 0.8 add_bitcast_fusion
  70.8 0.6 fusion.29
  71.4 0.4 copy.35
  71.8 0.4 copy.36
  72.4 28.6 %all_to_all.21 = bf16[32,8,16,128]{3,2,1,0:T(8,128)(2,1)S(1)} all-to-all(bf16[32,8,16,128]{3,2,1,0:T(8,128)(2,1)S(1)} %pad_maximum_fusion.1), channel_id=1, replica_groups=mesh['row'=16,'ch'=2] {'row','ch'}, dimensions={0} | all-to-all | bytes 2097152 | tf_op jit(solution)/shard_map/all_to_all | solution.py:137
  101.0 1.6 %copy.58 = bf16[16,2,8,16,128]{4,1,3,0,2:T(2,128)(2,1)S(1)} copy(bf16[16,2,8,16,128]{4,3,2,1,0:T(8,128)(2,1)S(1)} %bitcast.77) | data formatting | bytes 2097152 | tf_op jit(solution)/shard_map/reshape | solution.py:138
  102.6 0.8 fusion.58
  103.4 0.3 slice.137
  103.7 0.3 slice.139
  104.1 0.3 convolution_convert_fusion
  104.4 0.1 reshape.145
  104.6 0.9 copy.39
  105.5 3.8 %all-to-all-start.3 = ((bf16[32,4,16,128]{3,2,1,0:T(8,128)(2,1)}), bf16[32,4,16,128]{3,2,1,0:T(8,128)(2,1)S(1)}, u32[]{:S(2)}, u32[]{:S(2)}) async-start(bf16[32,4,16,128]{3,2,1,0:T(8,128)(2,1)} %bitcast.33), calls=%async_computation.3 | async-start | bytes 1048576 | tf_op jit(solution)/shard_map/all_to_all | solution.py:150
  109.3 0.1 mul.193
  109.5 0.5 fusion.7
  110.0 15.1 %all-to-all-done.3 = bf16[32,4,16,128]{3,2,1,0:T(8,128)(2,1)S(1)} async-done(((bf16[32,4,16,128]{3,2,1,0:T(8,128)(2,1)}), bf16[32,4,16,128]{3,2,1,0:T(8,128)(2,1)S(1)}, u32[]{:S(2)}, u32[]{:S(2)}) %all-to-all-start.3) | async-done | bytes 524320 | tf_op jit(solution)/shard_map/all_to_all | solution.py:150
  125.1 0.1 convert_reduce_fusion
  125.2 0.2 fusion.16
  125.4 0.3 fusion.19
  125.8 0.3 fusion.3
  126.2 1.3 %copy.42 = f32[16,128,128]{2,1,0:T(8,128)} copy(f32[16,128,128]{1,2,0:T(8,128)S(1)} %fusion.3) | data formatting | bytes 2097152 | tf_op jit(solution)/shard_map/add | solution.py:75
  (32 shorter events, 0.8 us)
Async XLA Ops:
  45.0 6.7 %copy-start = (f32[16,128,128]{2,1,0:T(8,128)S(1)}, f32[16,128,128]{2,1,0:T(8,128)}, u32[]{:S(2)}) copy-start(f32[16,128,128]{2,1,0:T(8,128)} %param.12) | copy-start | bytes 3145732
  46.1 5.9 %copy-start.4 = (f32[2,128]{1,0:T(2,128)S(1)}, f32[2,128]{1,0:T(2,128)}, u32[]{:S(2)}) copy-start(f32[2,128]{1,0:T(2,128)} %param.21) | copy-start | bytes 3076
  46.1 5.9 %copy-start.5 = (f32[2,128]{1,0:T(2,128)S(1)}, f32[2,128]{1,0:T(2,128)}, u32[]{:S(2)}) copy-start(f32[2,128]{1,0:T(2,128)} %param.20) | copy-start | bytes 3076
  46.1 6.1 %copy-start.3 = (f32[2,128]{1,0:T(2,128)S(1)}, f32[2,128]{1,0:T(2,128)}, u32[]{:S(2)}) copy-start(f32[2,128]{1,0:T(2,128)} %param.23) | copy-start | bytes 3076
  46.1 6.1 %copy-start.6 = (bf16[2,128,128]{2,1,0:T(8,128)(2,1)S(1)}, bf16[2,128,128]{2,1,0:T(8,128)(2,1)}, u32[]{:S(2)}) copy-start(bf16[2,128,128]{2,1,0:T(8,128)(2,1)} %param.18) | copy-start | bytes 196612
  47.9 19.6 %all-to-all-start.1 = ((bf16[32,4,16,128]{3,2,1,0:T(8,128)(2,1)}), bf16[32,4,16,128]{3,2,1,0:T(8,128)(2,1)S(1)}, u32[]{:S(2)}, u32[]{:S(2)}) async-start(bf16[32,4,16,128]{3,2,1,0:T(8,128)(2,1)} %bitcast.14), calls=%async_computation.1 | async-start | bytes 1048576 | tf_op jit(solution)/shard_map/all_to_all | solution.py:150
  52.0 16.2 %copy-start.2 = (bf16[2,128,128]{2,1,0:T(8,128)(2,1)S(1)}, bf16[2,128,128]{2,1,0:T(8,128)(2,1)}, u32[]{:S(2)}) copy-start(bf16[2,128,128]{2,1,0:T(8,128)(2,1)} %param.22) | copy-start | bytes 196612
  54.3 15.7 %copy-start.1 = (bf16[2,128,512]{2,1,0:T(8,128)(2,1)S(1)}, bf16[2,128,512]{2,1,0:T(8,128)(2,1)}, u32[]{:S(2)}) copy-start(bf16[2,128,512]{2,1,0:T(8,128)(2,1)} %param.16) | copy-start | bytes 786436
  105.5 19.6 %all-to-all-start.3 = ((bf16[32,4,16,128]{3,2,1,0:T(8,128)(2,1)}), bf16[32,4,16,128]{3,2,1,0:T(8,128)(2,1)S(1)}, u32[]{:S(2)}, u32[]{:S(2)}) async-start(bf16[32,4,16,128]{3,2,1,0:T(8,128)(2,1)} %bitcast.33), calls=%async_computation.3 | async-start | bytes 1048576 | tf_op jit(solution)/shard_map/all_to_all | solution.py:150

commit v2 on v0

--- a/solution.py
+++ b/solution.py
@@ -1,6 +1,8 @@
 import jax
 import jax.numpy as jnp
 from jax import lax
+from jax.experimental import pallas as pl
+from jax.experimental.pallas import tpu as pltpu
 from jax.sharding import PartitionSpec as P
 
 PAIR_EPSILON = 1e-05
@@ -50,6 +52,29 @@
         + gate_bias[section_index]
     )
     return (left_panel, right_panel, gate_value)
+
+
+def finish(
+    gathered,
+    current,
+    gate_value,
+    section_index,
+    hidden_gain,
+    hidden_shift,
+    output_weight,
+    output_bias,
+):
+    normed = layer_norm(
+        gathered,
+        hidden_gain[section_index][:, None, None],
+        hidden_shift[section_index][:, None, None],
+        0,
+        HIDDEN_EPSILON,
+    ).astype(jnp.bfloat16)
+    projected = jnp.einsum(
+        "hrj,hc->rjc", normed, output_weight[section_index], preferred_element_type=jnp.float32
+    )
+    return current + gate_value * (projected + output_bias[section_index])
 
 
 def local(
@@ -156,23 +181,307 @@
         gathered = jnp.transpose(gathered, (0, 1, 3, 2, 4, 5)).reshape(
             hidden_width, row_count, col_count
         )
-        normed = layer_norm(
+        current = finish(
             gathered,
-            hidden_gain[section_index][:, None, None],
-            hidden_shift[section_index][:, None, None],
-            0,
-            HIDDEN_EPSILON,
-        ).astype(jnp.bfloat16)
-        projected = jnp.einsum(
-            "hrj,hc->rjc", normed, output_weight[section_index], preferred_element_type=jnp.float32
-        )
-        current = current + gate_value * (projected + output_bias[section_index])
+            current,
+            gate_value,
+            section_index,
+            hidden_gain,
+            hidden_shift,
+            output_weight,
+            output_bias,
+        )
     return current
 
 
+CONTRACT_LAST = (((1,), (1,)), ((), ()))
+CONTRACT_FIRST = (((0,), (0,)), ((), ()))
+
+
+def spread(values, width):
+    return jnp.broadcast_to(values, (width, values.shape[1])).T
+
+
+def cell_row_mask(row_mask_ref, col_mask_ref, row):
+    first = lax.axis_index("row") * row_mask_ref.shape[0] // lax.axis_size("row")
+    col_mask = col_mask_ref[pl.ds(lax.axis_index("ch"), 1), :].astype(jnp.float32)
+    return row_mask_ref[first + row].astype(jnp.float32) * col_mask
+
+
+def project_setup(section, panel_weight_ref, panel_bias_ref, weight_ref, bias_ref):
+    weight_ref[...] = panel_weight_ref[section].astype(jnp.float32).T.astype(jnp.bfloat16)
+    bias_ref[...] = spread(panel_bias_ref[section : section + 1, :], bias_ref.shape[1])
+
+
+def project_row(
+    section, row, values, mask, gain_ref, shift_ref, weight_ref, bias_ref, normed_ref, panel_ref
+):
+    hidden = weight_ref.shape[0] // 4
+    normed = layer_norm(
+        values,
+        gain_ref[section : section + 1, :],
+        shift_ref[section : section + 1, :],
+        1,
+        PAIR_EPSILON,
+    ).astype(jnp.bfloat16)
+    normed_ref[row] = normed
+
+    def column(which):
+        part = pl.ds(which * hidden, hidden)
+        return (
+            lax.dot_general(
+                weight_ref[part, :], normed, CONTRACT_LAST, preferred_element_type=jnp.float32
+            )
+            + bias_ref[part, :]
+        )
+
+    panel_ref[row, :hidden] = mask * jax.nn.sigmoid(column(0)) * column(1)
+    panel_ref[row, hidden:] = mask * jax.nn.sigmoid(column(2)) * column(3)
+
+
+def pack_panels(panel_ref, send_ref):
+    own = send_ref.shape[1] // 2
+    hidden = panel_ref.shape[1] // 2
+    for side in range(2):
+        for first in range(0, hidden, 8):
+            block = panel_ref[:, side * hidden + first : side * hidden + first + 8, :]
+            block = jnp.transpose(block, (1, 0, 2)).astype(jnp.bfloat16)
+            for at in range(0, 8, own):
+                send_ref[(first + at) // own, side * own : (side + 1) * own] = block[at : at + own]
+
+
+def open_kernel(
+    section,
+    row_mask_ref,
+    col_mask_ref,
+    current_ref,
+    gain_ref,
+    shift_ref,
+    panel_weight_ref,
+    panel_bias_ref,
+    send_ref,
+    normed_ref,
+    weight_ref,
+    bias_ref,
+    panel_ref,
+):
+    project_setup(section, panel_weight_ref, panel_bias_ref, weight_ref, bias_ref)
+    for row in range(current_ref.shape[0]):
+        mask = cell_row_mask(row_mask_ref, col_mask_ref, row)
+        project_row(
+            section,
+            row,
+            current_ref[row],
+            mask,
+            gain_ref,
+            shift_ref,
+            weight_ref,
+            bias_ref,
+            normed_ref,
+            panel_ref,
+        )
+    pack_panels(panel_ref, send_ref)
+
+
+def product_kernel(section, got_ref, out_ref):
+    rows, cols, both, row_count, col_count = got_ref.shape
+    own = both // 2
+    total = rows * row_count
+
+    def load(col, index):
+        return got_ref[:, col, index].reshape(total, col_count)
+
+    for index in range(own):
+        left = [load(col, index) for col in range(cols)]
+        right = [load(col, own + index) for col in range(cols)]
+        if section == 0:
+            products = lax.dot_general(
+                jnp.concatenate(left, axis=1),
+                jnp.concatenate(right, axis=1),
+                CONTRACT_LAST,
+                preferred_element_type=jnp.float32,
+            )
+        else:
+            products = lax.dot_general(
+                jnp.concatenate(left, axis=1),
+                jnp.concatenate(right, axis=1),
+                CONTRACT_FIRST,
+                preferred_element_type=jnp.float32,
+            )
+        products = products.astype(jnp.bfloat16)
+        for col in range(cols):
+            out_ref[:, col, index] = products[:, col * col_count : (col + 1) * col_count].reshape(
+                rows, row_count, col_count
+            )
+
+
+def close_rows(
+    section,
+    gathered_ref,
+    current_ref,
+    normed_ref,
+    gate_weight_ref,
+    gate_bias_ref,
+    hidden_gain_ref,
+    hidden_shift_ref,
+    output_weight_ref,
+    output_bias_ref,
+    turned_ref,
+):
+    hidden, rows, width = gathered_ref.shape
+    values = gathered_ref[...].astype(jnp.float32)
+    center = jnp.mean(values, axis=0)
+    offset = values - center[None]
+    scale = lax.rsqrt(jnp.mean(offset * offset, axis=0) + HIDDEN_EPSILON)
+    for first in range(0, hidden, 8):
+        block = (gathered_ref[first : first + 8].astype(jnp.float32) - center[None]) * scale[None]
+        turned_ref[:, first : first + 8, :] = jnp.transpose(block, (1, 0, 2))
+    gain = spread(hidden_gain_ref[section : section + 1, :], width)
+    shift = spread(hidden_shift_ref[section : section + 1, :], width)
+    for row in range(rows):
+        hidden_normed = (turned_ref[row] * gain + shift).astype(jnp.bfloat16)
+        projected = lax.dot_general(
+            hidden_normed,
+            output_weight_ref[section],
+            CONTRACT_FIRST,
+            preferred_element_type=jnp.float32,
+        )
+        gate = jax.nn.sigmoid(
+            jnp.dot(
+                normed_ref[row], gate_weight_ref[section], preferred_element_type=jnp.float32
+            )
+            + gate_bias_ref[section : section + 1, :]
+        )
+        yield row, current_ref[row] + gate * (projected + output_bias_ref[section : section + 1, :])
+
+
+def close_kernel(section, *refs):
+    out_ref = refs[9]
+    for row, values in close_rows(section, *refs[:9], refs[10]):
+        out_ref[row] = values
+
+
+def middle_kernel(section, *refs):
+    row_mask_ref, col_mask_ref, gain_ref, shift_ref, panel_weight_ref, panel_bias_ref = refs[9:15]
+    out_ref, send_ref, normed_ref, turned_ref, weight_ref, bias_ref, panel_ref = refs[15:]
+    project_setup(section + 1, panel_weight_ref, panel_bias_ref, weight_ref, bias_ref)
+    for row, values in close_rows(section, *refs[:9], turned_ref):
+        out_ref[row] = values
+        project_row(
+            section + 1,
+            row,
+            values,
+            cell_row_mask(row_mask_ref, col_mask_ref, row),
+            gain_ref,
+            shift_ref,
+            weight_ref,
+            bias_ref,
+            normed_ref,
+            panel_ref,
+        )
+    pack_panels(panel_ref, send_ref)
+
+
+def local_direct(
+    pair_rep,
+    residue_mask,
+    pair_gain,
+    pair_shift,
+    panel_weight,
+    panel_bias,
+    gate_weight,
+    gate_bias,
+    hidden_gain,
+    hidden_shift,
+    output_weight,
+    output_bias,
+):
+    row_count, col_count, channels = pair_rep.shape
+    rows = lax.axis_size("row")
+    cols = lax.axis_size("ch")
+    devices = rows * cols
+    hidden = panel_weight.shape[2] // 4
+    own = hidden // devices
+    vmem = pl.BlockSpec(memory_space=pltpu.VMEM)
+    smem = pl.BlockSpec(memory_space=pltpu.SMEM)
+    shape = jax.ShapeDtypeStruct
+    send_shape = shape((devices, 2 * own, row_count, col_count), jnp.bfloat16)
+    normed_shape = shape((row_count, col_count, channels), jnp.bfloat16)
+    pair_shape = shape(pair_rep.shape, jnp.float32)
+    project_scratch = [
+        pltpu.VMEM((4 * hidden, channels), jnp.bfloat16),
+        pltpu.VMEM((4 * hidden, col_count), jnp.float32),
+        pltpu.VMEM((row_count, 2 * hidden, col_count), jnp.float32),
+    ]
+    close_scratch = [pltpu.VMEM((row_count, hidden, col_count), jnp.float32)]
+    col_mask = residue_mask.reshape(cols, col_count)
+
+    def exchange(values):
+        return lax.all_to_all(values, ("row", "ch"), split_axis=0, concat_axis=0, tiled=True)
+
+    def triangle(section, send):
+        got = exchange(send).reshape(rows, cols, 2 * own, row_count, col_count)
+        products = pl.pallas_call(
+            lambda *refs: product_kernel(section, *refs),
+            out_shape=shape((rows, cols, own, row_count, col_count), jnp.bfloat16),
+            in_specs=[vmem],
+            out_specs=vmem,
+            name=f"products_{section}",
+        )(got)
+        back = exchange(products.reshape(devices, own, row_count, col_count))
+        return back.reshape(hidden, row_count, col_count)
+
+    send, normed = pl.pallas_call(
+        lambda *refs: open_kernel(0, *refs),
+        out_shape=(send_shape, normed_shape),
+        in_specs=[smem] + [vmem] * 6,
+        out_specs=(vmem, vmem),
+        scratch_shapes=project_scratch,
+        name="open",
+    )(residue_mask, col_mask, pair_rep, pair_gain, pair_shift, panel_weight, panel_bias)
+    closing = (gate_weight, gate_bias, hidden_gain, hidden_shift, output_weight, output_bias)
+    gathered = triangle(0, send)
+    current, send, normed = pl.pallas_call(
+        lambda *refs: middle_kernel(0, *refs),
+        out_shape=(pair_shape, send_shape, normed_shape),
+        in_specs=[vmem] * 9 + [smem] + [vmem] * 5,
+        out_specs=(vmem, vmem, vmem),
+        scratch_shapes=close_scratch + project_scratch,
+        name="middle",
+    )(
+        gathered,
+        pair_rep,
+        normed,
+        *closing,
+        residue_mask,
+        col_mask,
+        pair_gain,
+        pair_shift,
+        panel_weight,
+        panel_bias,
+    )
+    gathered = triangle(1, send)
+    return pl.pallas_call(
+        lambda *refs: close_kernel(1, *refs),
+        out_shape=pair_shape,
+        in_specs=[vmem] * 9,
+        out_specs=vmem,
+        scratch_shapes=close_scratch,
+        name="close",
+    )(gathered, current, normed, *closing)
+
+
 def solution(mesh):
+    devices = mesh.shape["row"] * mesh.shape["ch"]
+
+    def body(*args):
+        hidden = args[4].shape[2] // 4
+        if hidden % devices == 0 and 8 % (hidden // devices) == 0 and args[0].shape[0] % 16 == 0:
+            return local_direct(*args)
+        return local(*args)
+
     return jax.shard_map(
-        local,
+        body,
         mesh=mesh,
         in_specs=(P("row", "ch", None), P(), P(), P(), P(), P(), P(), P(), P(), P(), P(), P()),
         out_specs=P("row", "ch", None),

time: 240 us -> 126 us (0.53)
  waiting for transfers between devices: 105 us -> 0 us
  starting transfers between devices: 43.3 us -> 0 us
  blocking collectives: 59.1 us -> 102 us
  Pallas kernels: 0 us -> 23.9 us
  local copies, waits for them, and re-layouts: 16.7 us -> 0 us
  matrix products: 6.9 us -> 0 us
  other arithmetic: 6.83 us -> 0 us
    all_to_all x10 -> x0, waiting for transfers between devices: 105 us -> none  [the longest x2 27.2 us: local(): lax.all_to_all(lax.all_to_all(send_right, 'ch', split_axis=0, concat_axis...]
    all_to_all x10 -> x0, starting transfers between devices: 43.3 us -> none  [the longest x2 12.3 us: local(): lax.all_to_all(lax.all_to_all(send_left, 'ch', split_axis=0, concat_axis=...]
    all_to_all x2 -> x4, blocking collectives: 59.1 us -> 102 us  [exchange(): lax.all_to_all(values, ('row', 'ch'), split_axis=0, concat_axis=0, tiled=...]
    pallas_call x0 -> x5, Pallas kernels: none -> 23.9 us  [the longest x1 10.5 us: local_direct(): pl.pallas_call(lambda *refs: middle_kernel(0, *refs), out_shape=(pair_sha...]
    dot_general x8 -> x0, matrix products: 6.9 us -> none  [the longest x2 2.99 us: project(): jnp.einsum('rjc,cf->frj', normed, panel_weight[section_index], preferred_...]
    all_to_all x10 -> x0, local copies, waits for them, and re-layouts: 5.7 us -> none  [the longest x2 2.11 us: local(): lax.all_to_all(returned, 'row', split_axis=1, concat_axis=0, tiled=True)]
    convert_element_type x4 -> x0, local copies, waits for them, and re-layouts: 4.74 us -> none  [the longest x2 2.38 us: project(): left_panel = (cell_mask * jax.nn.sigmoid(features[:hidden_width]) * featu...]
    reduce_sum x7 -> x0, other arithmetic: 4.14 us -> none  [the longest x4 2.3 us: layer_norm(): spread = jnp.mean(offset * offset, axis=along, keepdims=True)]
  transfers between devices with their start and end apart: 10 -> 0, of which waited for: 10 -> 0; matrix products, arithmetic and copies ran while one was open for 4% -> 0% of each run, Pallas kernels for 0% -> 0%
where the time goes in v2:
time: 126 us
  blocking collectives  102 us (81%)
  Pallas kernels  23.9 us (19%)
    all_to_all x4, blocking collectives, exchange(): lax.all_to_all(values, ('row', 'ch'), split_axis=0, concat_axis=0, tiled=...  102 us
    pallas_call x1, Pallas kernels, local_direct(): pl.pallas_call(lambda *refs: middle_kernel(0, *refs), out_shape=(pair_sha...  10.5 us
    pallas_call x1, Pallas kernels, local_direct(): pl.pallas_call(lambda *refs: open_kernel(0, *refs), out_shape=(send_shape...  5.11 us
    pallas_call x2, Pallas kernels, triangle(): pl.pallas_call(lambda *refs: product_kernel(section, *refs), out_shape=sh...  4.72 us
    pallas_call x1, Pallas kernels, local_direct(): pl.pallas_call(lambda *refs: close_kernel(1, *refs), out_shape=pair_shape...  3.56 us

profile of v2, /device:TPU:1, one launch (start us, length us, event | category | flops | bytes accessed | tf_op | source)
XLA Modules:
  0.0 125.5 jit_solution(5668826789986062110)
XLA Ops:
  0.0 5.1 %open.1 = (bf16[32,8,16,128]{3,2,1,0:T(8,128)(2,1)}, bf16[16,128,128]{2,1,0:T(8,128)(2,1)}) custom-call(s32[256]{0:T(256)} %refs_9_.1, s32[2,128]{1,0:T(2,128)} %bitcast.13, f32[16,128,128]{2,1,0:T(8,128)} %refs_1_.1, f32[2,128]{1,0:T(2,128)} %refs_11_.1, f32[2,128]{1,0:T(2,128)} %refs_12_.1, bf16[2,128,512]{2,1,0:T(8,128)(2,1)} %refs_13_.1, f32[2,512]{1,0:T(2,128)} %refs_14_.1), custom_call_target="tpu_custom_call" | custom-call | tf_op jit(solution)/shard_map/open/pallas_call | solution.py:434
  5.1 33.3 %all_to_all.20 = bf16[32,8,16,128]{3,2,1,0:T(8,128)(2,1)} all-to-all(bf16[32,8,16,128]{3,2,1,0:T(8,128)(2,1)} %get-tuple-element.10), channel_id=1, replica_groups=mesh['row'=16,'ch'=2] {'row','ch'}, dimensions={0} | all-to-all | bytes 2097152 | tf_op jit(solution)/shard_map/all_to_all | solution.py:420
  38.4 2.3 %products_0.1 = bf16[16,2,4,16,128]{4,3,2,1,0:T(8,128)(2,1)} custom-call(bf16[16,2,8,16,128]{4,3,2,1,0:T(8,128)(2,1)} %bitcast.7), custom_call_target="tpu_custom_call" | custom-call | tf_op jit(solution)/shard_map/products_0/pallas_call | solution.py:424
  40.7 19.7 %all_to_all.21 = bf16[32,4,16,128]{3,2,1,0:T(8,128)(2,1)} all-to-all(bf16[32,4,16,128]{3,2,1,0:T(8,128)(2,1)} %bitcast.11), channel_id=1, replica_groups=mesh['row'=16,'ch'=2] {'row','ch'}, dimensions={0} | all-to-all | bytes 1048576 | tf_op jit(solution)/shard_map/all_to_all | solution.py:420
  60.4 10.5 %middle.1 = (f32[16,128,128]{2,1,0:T(8,128)}, bf16[32,8,16,128]{3,2,1,0:T(8,128)(2,1)}, bf16[16,128,128]{2,1,0:T(8,128)(2,1)}) custom-call(bf16[128,16,128]{2,1,0:T(8,128)(2,1)} %bitcast.9, f32[16,128,128]{2,1,0:T(8,128)} %refs_1_.1, bf16[16,128,128]{2,1,0:T(8,128)(2,1)} %get-tuple-element.11.refs_2_, bf16[2,128,128]{2,1,0:T(8,128)(2,1)} %refs_3_.5, ...), custom_call_target="tpu_custom_call" | custom-call | tf_op jit(solution)/shard_map/middle/pallas_call | solution.py:444
  71.0 28.9 %all_to_all.22 = bf16[32,8,16,128]{3,2,1,0:T(8,128)(2,1)} all-to-all(bf16[32,8,16,128]{3,2,1,0:T(8,128)(2,1)} %get-tuple-element.12), channel_id=1, replica_groups=mesh['row'=16,'ch'=2] {'row','ch'}, dimensions={0} | all-to-all | bytes 2097152 | tf_op jit(solution)/shard_map/all_to_all | solution.py:420
  99.9 2.4 %products_1.1 = bf16[16,2,4,16,128]{4,3,2,1,0:T(8,128)(2,1)} custom-call(bf16[16,2,8,16,128]{4,3,2,1,0:T(8,128)(2,1)} %bitcast.8), custom_call_target="tpu_custom_call" | custom-call | tf_op jit(solution)/shard_map/products_1/pallas_call | solution.py:424
  102.3 19.7 %all_to_all.23 = bf16[32,4,16,128]{3,2,1,0:T(8,128)(2,1)} all-to-all(bf16[32,4,16,128]{3,2,1,0:T(8,128)(2,1)} %bitcast.12), channel_id=1, replica_groups=mesh['row'=16,'ch'=2] {'row','ch'}, dimensions={0} | all-to-all | bytes 1048576 | tf_op jit(solution)/shard_map/all_to_all | solution.py:420
  122.0 3.6 %close.1 = f32[16,128,128]{2,1,0:T(8,128)} custom-call(bf16[128,16,128]{2,1,0:T(8,128)(2,1)} %bitcast.10, f32[16,128,128]{2,1,0:T(8,128)} %get-tuple-element.13.refs_1_, bf16[16,128,128]{2,1,0:T(8,128)(2,1)} %get-tuple-element.14.refs_2_, bf16[2,128,128]{2,1,0:T(8,128)(2,1)} %refs_3_.5, f32[2,128]{1,0:T(2,128)} %refs_4_.5, f32[2,128]{1,0:T(2,128)} %refs_5_.5, ...), custom_call_target="tpu_custom_call" | custom-call | tf_op jit(solution)/shard_map/close/pallas_call | solution.py:464

commit v3 on v2

--- a/solution.py
+++ b/solution.py
@@ -209,34 +209,54 @@
 
 
 def project_setup(section, panel_weight_ref, panel_bias_ref, weight_ref, bias_ref):
-    weight_ref[...] = panel_weight_ref[section].astype(jnp.float32).T.astype(jnp.bfloat16)
-    bias_ref[...] = spread(panel_bias_ref[section : section + 1, :], bias_ref.shape[1])
-
-
-def project_row(
-    section, row, values, mask, gain_ref, shift_ref, weight_ref, bias_ref, normed_ref, panel_ref
-):
     hidden = weight_ref.shape[0] // 4
-    normed = layer_norm(
-        values,
-        gain_ref[section : section + 1, :],
-        shift_ref[section : section + 1, :],
-        1,
-        PAIR_EPSILON,
-    ).astype(jnp.bfloat16)
-    normed_ref[row] = normed
+    for which in range(4):
+        part = slice(which * hidden, (which + 1) * hidden)
+        factor = 0.5 if which % 2 == 0 else 1.0
+        weight = panel_weight_ref[section, :, part].astype(jnp.float32) * factor
+        weight_ref[part, :] = weight.T.astype(jnp.bfloat16)
+        bias_ref[part, :] = spread(
+            panel_bias_ref[section : section + 1, part] * factor, bias_ref.shape[1]
+        )
+
+
+def project_rows(
+    section, row, values, masks, gain_ref, shift_ref, weight_ref, bias_ref, normed_ref, panel_ref
+):
+    hidden = weight_ref.shape[0] // 4
+    width = panel_ref.shape[2]
+    normed = []
+    for at, value in enumerate(values):
+        normed.append(
+            layer_norm(
+                value,
+                gain_ref[section : section + 1, :],
+                shift_ref[section : section + 1, :],
+                1,
+                PAIR_EPSILON,
+            ).astype(jnp.bfloat16)
+        )
+        normed_ref[row + at] = normed[at]
+    cells = jnp.concatenate(normed, axis=0)
 
     def column(which):
-        part = pl.ds(which * hidden, hidden)
-        return (
-            lax.dot_general(
-                weight_ref[part, :], normed, CONTRACT_LAST, preferred_element_type=jnp.float32
-            )
-            + bias_ref[part, :]
-        )
-
-    panel_ref[row, :hidden] = mask * jax.nn.sigmoid(column(0)) * column(1)
-    panel_ref[row, hidden:] = mask * jax.nn.sigmoid(column(2)) * column(3)
+        return lax.dot_general(
+            weight_ref[which * hidden : (which + 1) * hidden, :],
+            cells,
+            CONTRACT_LAST,
+            preferred_element_type=jnp.float32,
+        )
+
+    for side in range(2):
+        gates = column(2 * side)
+        panel = column(2 * side + 1)
+        gate_bias = bias_ref[2 * side * hidden : (2 * side + 1) * hidden, :]
+        panel_bias = bias_ref[(2 * side + 1) * hidden : (2 * side + 2) * hidden, :]
+        for at in range(len(values)):
+            lanes = slice(at * width, (at + 1) * width)
+            turn = jnp.tanh(gates[:, lanes] + gate_bias)
+            half = (0.5 * masks[at]) * (panel[:, lanes] + panel_bias)
+            panel_ref[row + at, side * hidden : (side + 1) * hidden] = half + half * turn
 
 
 def pack_panels(panel_ref, send_ref):
@@ -266,13 +286,12 @@
     panel_ref,
 ):
     project_setup(section, panel_weight_ref, panel_bias_ref, weight_ref, bias_ref)
-    for row in range(current_ref.shape[0]):
-        mask = cell_row_mask(row_mask_ref, col_mask_ref, row)
-        project_row(
+    for row in range(0, current_ref.shape[0], 2):
+        project_rows(
             section,
             row,
-            current_ref[row],
-            mask,
+            [current_ref[row], current_ref[row + 1]],
+            [cell_row_mask(row_mask_ref, col_mask_ref, row + at) for at in range(2)],
             gain_ref,
             shift_ref,
             weight_ref,
@@ -329,36 +348,47 @@
     turned_ref,
 ):
     hidden, rows, width = gathered_ref.shape
-    values = gathered_ref[...].astype(jnp.float32)
-    center = jnp.mean(values, axis=0)
-    offset = values - center[None]
-    scale = lax.rsqrt(jnp.mean(offset * offset, axis=0) + HIDDEN_EPSILON)
-    for first in range(0, hidden, 8):
-        block = (gathered_ref[first : first + 8].astype(jnp.float32) - center[None]) * scale[None]
-        turned_ref[:, first : first + 8, :] = jnp.transpose(block, (1, 0, 2))
+    firsts = range(0, hidden, 8)
+
+    def block(first):
+        return gathered_ref[first : first + 8].astype(jnp.float32)
+
+    center = sum(jnp.sum(block(first), axis=0) for first in firsts) / hidden
+    spread_sum = sum(jnp.sum((block(first) - center[None]) ** 2, axis=0) for first in firsts)
+    scale = lax.rsqrt(spread_sum / hidden + HIDDEN_EPSILON)
+    for first in firsts:
+        turned_ref[:, first : first + 8, :] = jnp.transpose(
+            (block(first) - center[None]) * scale[None], (1, 0, 2)
+        )
     gain = spread(hidden_gain_ref[section : section + 1, :], width)
     shift = spread(hidden_shift_ref[section : section + 1, :], width)
-    for row in range(rows):
-        hidden_normed = (turned_ref[row] * gain + shift).astype(jnp.bfloat16)
-        projected = lax.dot_general(
-            hidden_normed,
-            output_weight_ref[section],
-            CONTRACT_FIRST,
-            preferred_element_type=jnp.float32,
-        )
-        gate = jax.nn.sigmoid(
-            jnp.dot(
-                normed_ref[row], gate_weight_ref[section], preferred_element_type=jnp.float32
-            )
-            + gate_bias_ref[section : section + 1, :]
-        )
-        yield row, current_ref[row] + gate * (projected + output_bias_ref[section : section + 1, :])
+    output_bias = output_bias_ref[section : section + 1, :]
+    gate_weight = (gate_weight_ref[section].astype(jnp.float32) * 0.5).astype(jnp.bfloat16)
+    gate_bias = gate_bias_ref[section : section + 1, :] * 0.5
+    for row in range(0, rows, 2):
+        pair = []
+        for at in range(2):
+            hidden_normed = (turned_ref[row + at] * gain + shift).astype(jnp.bfloat16)
+            projected = lax.dot_general(
+                hidden_normed,
+                output_weight_ref[section],
+                CONTRACT_FIRST,
+                preferred_element_type=jnp.float32,
+            )
+            turn = jnp.tanh(
+                jnp.dot(normed_ref[row + at], gate_weight, preferred_element_type=jnp.float32)
+                + gate_bias
+            )
+            half = 0.5 * (projected + output_bias)
+            pair.append(current_ref[row + at] + (half + half * turn))
+        yield row, pair
 
 
 def close_kernel(section, *refs):
     out_ref = refs[9]
     for row, values in close_rows(section, *refs[:9], refs[10]):
-        out_ref[row] = values
+        out_ref[row] = values[0]
+        out_ref[row + 1] = values[1]
 
 
 def middle_kernel(section, *refs):
@@ -366,12 +396,13 @@
     out_ref, send_ref, normed_ref, turned_ref, weight_ref, bias_ref, panel_ref = refs[15:]
     project_setup(section + 1, panel_weight_ref, panel_bias_ref, weight_ref, bias_ref)
     for row, values in close_rows(section, *refs[:9], turned_ref):
-        out_ref[row] = values
-        project_row(
+        out_ref[row] = values[0]
+        out_ref[row + 1] = values[1]
+        project_rows(
             section + 1,
             row,
             values,
-            cell_row_mask(row_mask_ref, col_mask_ref, row),
+            [cell_row_mask(row_mask_ref, col_mask_ref, row + at) for at in range(2)],
             gain_ref,
             shift_ref,
             weight_ref,

time: 126 us -> 122 us (0.968)
  Pallas kernels: 23.9 us -> 20.1 us
    pallas_call x1, Pallas kernels: 10.5 us -> 7.45 us  [local_direct(): pl.pallas_call(lambda *refs: middle_kernel(0, *refs), out_shape=(pair_sha...]
where the time goes in v3:
time: 122 us
  blocking collectives  102 us (84%)
  Pallas kernels  20.1 us (16%)
    all_to_all x4, blocking collectives, exchange(): lax.all_to_all(values, ('row', 'ch'), split_axis=0, concat_axis=0, tiled=...  102 us
    pallas_call x1, Pallas kernels, local_direct(): pl.pallas_call(lambda *refs: middle_kernel(0, *refs), out_shape=(pair_sha...  7.45 us
    pallas_call x2, Pallas kernels, triangle(): pl.pallas_call(lambda *refs: product_kernel(section, *refs), out_shape=sh...  4.73 us
    pallas_call x1, Pallas kernels, local_direct(): pl.pallas_call(lambda *refs: open_kernel(0, *refs), out_shape=(send_shape...  4.47 us
    pallas_call x1, Pallas kernels, local_direct(): pl.pallas_call(lambda *refs: close_kernel(1, *refs), out_shape=pair_shape...  3.48 us

profile of v3, /device:TPU:1, one launch (start us, length us, event | category | flops | bytes accessed | tf_op | source)
XLA Modules:
  0.0 121.8 jit_solution(8135087894182692248)
XLA Ops:
  0.0 4.5 %open.1 = (bf16[32,8,16,128]{3,2,1,0:T(8,128)(2,1)}, bf16[16,128,128]{2,1,0:T(8,128)(2,1)}) custom-call(s32[256]{0:T(256)} %refs_9_.1, s32[2,128]{1,0:T(2,128)} %bitcast.13, f32[16,128,128]{2,1,0:T(8,128)} %refs_1_.1, f32[2,128]{1,0:T(2,128)} %refs_11_.1, f32[2,128]{1,0:T(2,128)} %refs_12_.1, bf16[2,128,512]{2,1,0:T(8,128)(2,1)} %refs_13_.1, f32[2,512]{1,0:T(2,128)} %refs_14_.1), custom_call_target="tpu_custom_call" | custom-call | tf_op jit(solution)/shard_map/open/pallas_call | solution.py:465
  4.5 33.3 %all_to_all.20 = bf16[32,8,16,128]{3,2,1,0:T(8,128)(2,1)} all-to-all(bf16[32,8,16,128]{3,2,1,0:T(8,128)(2,1)} %get-tuple-element.10), channel_id=1, replica_groups=mesh['row'=16,'ch'=2] {'row','ch'}, dimensions={0} | all-to-all | bytes 2097152 | tf_op jit(solution)/shard_map/all_to_all | solution.py:451
  37.7 2.4 %products_0.1 = bf16[16,2,4,16,128]{4,3,2,1,0:T(8,128)(2,1)} custom-call(bf16[16,2,8,16,128]{4,3,2,1,0:T(8,128)(2,1)} %bitcast.7), custom_call_target="tpu_custom_call" | custom-call | tf_op jit(solution)/shard_map/products_0/pallas_call | solution.py:455
  40.1 19.7 %all_to_all.21 = bf16[32,4,16,128]{3,2,1,0:T(8,128)(2,1)} all-to-all(bf16[32,4,16,128]{3,2,1,0:T(8,128)(2,1)} %bitcast.11), channel_id=1, replica_groups=mesh['row'=16,'ch'=2] {'row','ch'}, dimensions={0} | all-to-all | bytes 1048576 | tf_op jit(solution)/shard_map/all_to_all | solution.py:451
  59.8 7.5 %middle.1 = (f32[16,128,128]{2,1,0:T(8,128)}, bf16[32,8,16,128]{3,2,1,0:T(8,128)(2,1)}, bf16[16,128,128]{2,1,0:T(8,128)(2,1)}) custom-call(bf16[128,16,128]{2,1,0:T(8,128)(2,1)} %bitcast.9, f32[16,128,128]{2,1,0:T(8,128)} %refs_1_.1, bf16[16,128,128]{2,1,0:T(8,128)(2,1)} %get-tuple-element.11.refs_2_, bf16[2,128,128]{2,1,0:T(8,128)(2,1)} %refs_3_.5, ...), custom_call_target="tpu_custom_call" | custom-call | tf_op jit(solution)/shard_map/middle/pallas_call | solution.py:475
  67.3 28.9 %all_to_all.22 = bf16[32,8,16,128]{3,2,1,0:T(8,128)(2,1)} all-to-all(bf16[32,8,16,128]{3,2,1,0:T(8,128)(2,1)} %get-tuple-element.12), channel_id=1, replica_groups=mesh['row'=16,'ch'=2] {'row','ch'}, dimensions={0} | all-to-all | bytes 2097152 | tf_op jit(solution)/shard_map/all_to_all | solution.py:451
  96.2 2.4 %products_1.1 = bf16[16,2,4,16,128]{4,3,2,1,0:T(8,128)(2,1)} custom-call(bf16[16,2,8,16,128]{4,3,2,1,0:T(8,128)(2,1)} %bitcast.8), custom_call_target="tpu_custom_call" | custom-call | tf_op jit(solution)/shard_map/products_1/pallas_call | solution.py:455
  98.6 19.7 %all_to_all.23 = bf16[32,4,16,128]{3,2,1,0:T(8,128)(2,1)} all-to-all(bf16[32,4,16,128]{3,2,1,0:T(8,128)(2,1)} %bitcast.12), channel_id=1, replica_groups=mesh['row'=16,'ch'=2] {'row','ch'}, dimensions={0} | all-to-all | bytes 1048576 | tf_op jit(solution)/shard_map/all_to_all | solution.py:451
  118.3 3.5 %close.1 = f32[16,128,128]{2,1,0:T(8,128)} custom-call(bf16[128,16,128]{2,1,0:T(8,128)(2,1)} %bitcast.10, f32[16,128,128]{2,1,0:T(8,128)} %get-tuple-element.13.refs_1_, bf16[16,128,128]{2,1,0:T(8,128)(2,1)} %get-tuple-element.14.refs_2_, bf16[2,128,128]{2,1,0:T(8,128)(2,1)} %refs_3_.5, f32[2,128]{1,0:T(2,128)} %refs_4_.5, f32[2,128]{1,0:T(2,128)} %refs_5_.5, ...), custom_call_target="tpu_custom_call" | custom-call | tf_op jit(solution)/shard_map/close/pallas_call | solution.py:495

commit v4 on v3

--- a/solution.py
+++ b/solution.py
@@ -7,6 +7,7 @@
 
 PAIR_EPSILON = 1e-05
 HIDDEN_EPSILON = 1.0
+GRANT = 32 * 1024 * 1024
 
 
 def layer_norm(values, gain_value, shift_value, along, epsilon):
@@ -436,9 +437,10 @@
     vmem = pl.BlockSpec(memory_space=pltpu.VMEM)
     smem = pl.BlockSpec(memory_space=pltpu.SMEM)
     shape = jax.ShapeDtypeStruct
-    send_shape = shape((devices, 2 * own, row_count, col_count), jnp.bfloat16)
-    normed_shape = shape((row_count, col_count, channels), jnp.bfloat16)
+    send_shape = pltpu.VMEM((devices, 2 * own, row_count, col_count), jnp.bfloat16)
     pair_shape = shape(pair_rep.shape, jnp.float32)
+    normed_kept = pltpu.VMEM((row_count, col_count, channels), jnp.bfloat16)
+    pair_kept = pltpu.VMEM(pair_rep.shape, jnp.float32)
     project_scratch = [
         pltpu.VMEM((4 * hidden, channels), jnp.bfloat16),
         pltpu.VMEM((4 * hidden, col_count), jnp.float32),
@@ -452,43 +454,58 @@
 
     def triangle(section, send):
         got = exchange(send).reshape(rows, cols, 2 * own, row_count, col_count)
+        got = pltpu.with_memory_space_constraint(got, pltpu.VMEM)
         products = pl.pallas_call(
             lambda *refs: product_kernel(section, *refs),
-            out_shape=shape((rows, cols, own, row_count, col_count), jnp.bfloat16),
+            out_shape=pltpu.VMEM((rows, cols, own, row_count, col_count), jnp.bfloat16),
             in_specs=[vmem],
             out_specs=vmem,
+            compiler_params=pltpu.CompilerParams(vmem_limit_bytes=GRANT),
             name=f"products_{section}",
         )(got)
         back = exchange(products.reshape(devices, own, row_count, col_count))
-        return back.reshape(hidden, row_count, col_count)
+        back = back.reshape(hidden, row_count, col_count)
+        return pltpu.with_memory_space_constraint(back, pltpu.VMEM)
 
     send, normed = pl.pallas_call(
         lambda *refs: open_kernel(0, *refs),
-        out_shape=(send_shape, normed_shape),
+        out_shape=(send_shape, normed_kept),
         in_specs=[smem] + [vmem] * 6,
         out_specs=(vmem, vmem),
         scratch_shapes=project_scratch,
+        compiler_params=pltpu.CompilerParams(vmem_limit_bytes=GRANT),
         name="open",
-    )(residue_mask, col_mask, pair_rep, pair_gain, pair_shift, panel_weight, panel_bias)
+    )(
+        residue_mask,
+        *(
+            pltpu.with_memory_space_constraint(values, pltpu.HBM)
+            for values in (col_mask, pair_rep, pair_gain, pair_shift, panel_weight, panel_bias)
+        ),
+    )
+    def keep(values):
+        return pltpu.with_memory_space_constraint(values, pltpu.VMEM)
+
     closing = (gate_weight, gate_bias, hidden_gain, hidden_shift, output_weight, output_bias)
+    closing = tuple(keep(values) for values in closing)
     gathered = triangle(0, send)
     current, send, normed = pl.pallas_call(
         lambda *refs: middle_kernel(0, *refs),
-        out_shape=(pair_shape, send_shape, normed_shape),
+        out_shape=(pair_kept, send_shape, normed_kept),
         in_specs=[vmem] * 9 + [smem] + [vmem] * 5,
         out_specs=(vmem, vmem, vmem),
         scratch_shapes=close_scratch + project_scratch,
+        compiler_params=pltpu.CompilerParams(vmem_limit_bytes=GRANT),
         name="middle",
     )(
         gathered,
-        pair_rep,
-        normed,
+        keep(pair_rep),
+        keep(normed),
         *closing,
         residue_mask,
         col_mask,
         pair_gain,
         pair_shift,
-        panel_weight,
+        keep(panel_weight),
         panel_bias,
     )
     gathered = triangle(1, send)
@@ -498,8 +515,9 @@
         in_specs=[vmem] * 9,
         out_specs=vmem,
         scratch_shapes=close_scratch,
+        compiler_params=pltpu.CompilerParams(vmem_limit_bytes=GRANT),
         name="close",
-    )(gathered, current, normed, *closing)
+    )(gathered, keep(current), keep(normed), *closing)
 
 
 def solution(mesh):

time: 122 us -> 113 us (0.926)
  Pallas kernels: 20.1 us -> 11.2 us
  blocking collectives: 102 us -> 100 us
    pallas_call x3, Pallas kernels: 12.2 us -> 5.82 us  [the longest x1 5.15 us: local_direct(): pl.pallas_call(lambda *refs: middle_kernel(0, *refs), out_shape=(pair_kep...]
    pallas_call x1, Pallas kernels: 3.48 us -> 1.93 us  [local_direct(): pl.pallas_call(lambda *refs: close_kernel(1, *refs), out_shape=pair_shape...]
where the time goes in v4:
time: 113 us; the launch traced here: 112 us
  blocking collectives  100 us (88%)
  Pallas kernels  11.2 us (10%)
    all_to_all x4, blocking collectives, exchange(): lax.all_to_all(values, ('row', 'ch'), split_axis=0, concat_axis=0, tiled=...  100 us
    pallas_call x1, Pallas kernels, local_direct(): pl.pallas_call(lambda *refs: middle_kernel(0, *refs), out_shape=(pair_kep...  5.15 us
    pallas_call x1, Pallas kernels, local_direct(): pl.pallas_call(lambda *refs: open_kernel(0, *refs), out_shape=(send_shape...  3.49 us

profile of v4, /device:TPU:1, one launch (start us, length us, event | category | flops | bytes accessed | tf_op | source)
XLA Modules:
  0.0 112.5 jit_solution(11201017248382243897)
XLA Ops:
  0.0 3.5 %open.1 = (bf16[32,8,16,128]{3,2,1,0:T(8,128)(2,1)S(1)}, bf16[16,128,128]{2,1,0:T(8,128)(2,1)S(1)}) custom-call(s32[256]{0:T(256)} %refs_9_.1, s32[2,128]{1,0:T(2,128)} %bitcast.13, f32[16,128,128]{2,1,0:T(8,128)} %refs_1_.1, f32[2,128]{1,0:T(2,128)} %refs_11_.1, f32[2,128]{1,0:T(2,128)} %refs_12_.1, bf16[2,128,512]{2,1,0:T(8,128)(2,1)} %refs_13_.1, ...), custom_call_target="tpu_custom_call" | custom-call | tf_op jit(solution)/shard_map/open/pallas_call | solution.py:470
  3.5 33.0 %all_to_all.20 = bf16[32,8,16,128]{3,2,1,0:T(8,128)(2,1)S(1)} all-to-all(bf16[32,8,16,128]{3,2,1,0:T(8,128)(2,1)S(1)} %get-tuple-element.10), channel_id=1, replica_groups=mesh['row'=16,'ch'=2] {'row','ch'}, dimensions={0} | all-to-all | bytes 2097152 | tf_op jit(solution)/shard_map/all_to_all | solution.py:453
  36.5 0.0 copy-start
  36.5 0.3 products_0.1
  36.8 0.0 copy-start.1
  36.8 0.0 copy-start.2
  36.8 0.0 copy-start.3
  36.8 0.0 copy-start.5
  36.8 0.0 copy-start.6
  36.9 0.0 copy-start.7
  36.9 0.0 copy-start.8
  36.9 0.0 copy-start.9
  36.9 0.0 copy-start.10
  36.9 0.0 copy-start.11
  36.9 19.4 %all_to_all.21 = bf16[32,4,16,128]{3,2,1,0:T(8,128)(2,1)S(1)} all-to-all(bf16[32,4,16,128]{3,2,1,0:T(8,128)(2,1)S(1)} %bitcast.11), channel_id=1, replica_groups=mesh['row'=16,'ch'=2] {'row','ch'}, dimensions={0} | all-to-all | bytes 1048576 | tf_op jit(solution)/shard_map/all_to_all | solution.py:453
  56.3 0.0 copy-start.4
  56.3 0.0 copy-done
  56.3 0.0 copy-done.1
  56.3 0.0 copy-done.2
  56.3 0.0 copy-done.3
  56.4 0.0 copy-done.5
  56.4 0.0 copy-done.6
  56.4 0.0 copy-done.7
  56.4 0.0 copy-done.8
  56.4 0.0 copy-done.9
  56.4 0.0 copy-done.10
  56.4 0.0 copy-done.11
  56.4 0.6 copy-done.4
  57.0 5.1 %middle.1 = (f32[16,128,128]{2,1,0:T(8,128)S(1)}, bf16[32,8,16,128]{3,2,1,0:T(8,128)(2,1)S(1)}, bf16[16,128,128]{2,1,0:T(8,128)(2,1)S(1)}) custom-call(bf16[128,16,128]{2,1,0:T(8,128)(2,1)S(1)} %bitcast.9, f32[16,128,128]{2,1,0:T(8,128)S(1)} %copy-done, bf16[16,128,128]{2,1,0:T(8,128)(2,1)S(1)} %get-tuple-element.11.refs_2_, ...), custom_call_target="tpu_custom_call" | custom-call | tf_op jit(solution)/shard_map/middle/pallas_call | solution.py:491
  62.2 28.6 %all_to_all.22 = bf16[32,8,16,128]{3,2,1,0:T(8,128)(2,1)S(1)} all-to-all(bf16[32,8,16,128]{3,2,1,0:T(8,128)(2,1)S(1)} %get-tuple-element.12), channel_id=1, replica_groups=mesh['row'=16,'ch'=2] {'row','ch'}, dimensions={0} | all-to-all | bytes 2097152 | tf_op jit(solution)/shard_map/all_to_all | solution.py:453
  90.8 0.3 products_1.1
  91.1 19.4 %all_to_all.23 = bf16[32,4,16,128]{3,2,1,0:T(8,128)(2,1)S(1)} all-to-all(bf16[32,4,16,128]{3,2,1,0:T(8,128)(2,1)S(1)} %bitcast.12), channel_id=1, replica_groups=mesh['row'=16,'ch'=2] {'row','ch'}, dimensions={0} | all-to-all | bytes 1048576 | tf_op jit(solution)/shard_map/all_to_all | solution.py:453
  110.6 1.9 %close.1 = f32[16,128,128]{2,1,0:T(8,128)} custom-call(bf16[128,16,128]{2,1,0:T(8,128)(2,1)S(1)} %bitcast.10, f32[16,128,128]{2,1,0:T(8,128)S(1)} %get-tuple-element.13.refs_1_, bf16[16,128,128]{2,1,0:T(8,128)(2,1)S(1)} %get-tuple-element.14.refs_2_, bf16[2,128,128]{2,1,0:T(8,128)(2,1)S(1)} %copy-done.2, f32[2,128]{1,0:T(2,128)S(1)} %copy-done.6, ...), custom_call_target="tpu_custom_call" | custom-call | tf_op jit(solution)/shard_map/close/pallas_call | solution.py:512
Async XLA Ops:
  36.5 19.9 %copy-start = (f32[16,128,128]{2,1,0:T(8,128)S(1)}, f32[16,128,128]{2,1,0:T(8,128)}, u32[]{:S(2)}) copy-start(f32[16,128,128]{2,1,0:T(8,128)} %refs_1_.1) | copy-start | bytes 3145732
  36.8 19.5 %copy-start.1 = (bf16[2,128,512]{2,1,0:T(8,128)(2,1)S(1)}, bf16[2,128,512]{2,1,0:T(8,128)(2,1)}, u32[]{:S(2)}) copy-start(bf16[2,128,512]{2,1,0:T(8,128)(2,1)} %refs_13_.1) | copy-start | bytes 786436
  36.8 19.5 %copy-start.2 = (bf16[2,128,128]{2,1,0:T(8,128)(2,1)S(1)}, bf16[2,128,128]{2,1,0:T(8,128)(2,1)}, u32[]{:S(2)}) copy-start(bf16[2,128,128]{2,1,0:T(8,128)(2,1)} %refs_3_.5) | copy-start | bytes 196612
  36.8 19.5 %copy-start.3 = (bf16[2,128,128]{2,1,0:T(8,128)(2,1)S(1)}, bf16[2,128,128]{2,1,0:T(8,128)(2,1)}, u32[]{:S(2)}) copy-start(bf16[2,128,128]{2,1,0:T(8,128)(2,1)} %refs_7_.3) | copy-start | bytes 196612
  36.8 19.5 %copy-start.5 = (f32[2,512]{1,0:T(2,128)S(1)}, f32[2,512]{1,0:T(2,128)}, u32[]{:S(2)}) copy-start(f32[2,512]{1,0:T(2,128)} %refs_14_.1) | copy-start | bytes 12292
  36.8 19.5 %copy-start.6 = (f32[2,128]{1,0:T(2,128)S(1)}, f32[2,128]{1,0:T(2,128)}, u32[]{:S(2)}) copy-start(f32[2,128]{1,0:T(2,128)} %refs_4_.5) | copy-start | bytes 3076
  36.9 19.5 %copy-start.7 = (f32[2,128]{1,0:T(2,128)S(1)}, f32[2,128]{1,0:T(2,128)}, u32[]{:S(2)}) copy-start(f32[2,128]{1,0:T(2,128)} %refs_5_.5) | copy-start | bytes 3076
  36.9 19.5 %copy-start.8 = (f32[2,128]{1,0:T(2,128)S(1)}, f32[2,128]{1,0:T(2,128)}, u32[]{:S(2)}) copy-start(f32[2,128]{1,0:T(2,128)} %refs_6_.5) | copy-start | bytes 3076
  36.9 19.5 %copy-start.9 = (f32[2,128]{1,0:T(2,128)S(1)}, f32[2,128]{1,0:T(2,128)}, u32[]{:S(2)}) copy-start(f32[2,128]{1,0:T(2,128)} %refs_8_.3) | copy-start | bytes 3076
  36.9 19.5 %copy-start.10 = (f32[2,128]{1,0:T(2,128)S(1)}, f32[2,128]{1,0:T(2,128)}, u32[]{:S(2)}) copy-start(f32[2,128]{1,0:T(2,128)} %refs_11_.1) | copy-start | bytes 3076
  36.9 19.5 %copy-start.11 = (f32[2,128]{1,0:T(2,128)S(1)}, f32[2,128]{1,0:T(2,128)}, u32[]{:S(2)}) copy-start(f32[2,128]{1,0:T(2,128)} %refs_12_.1) | copy-start | bytes 3076
  56.3 0.7 copy-start.4
